TPU v7x, 32 devices: a whole 2x2x4 slice. The times are simulated.
32 devices in a mesh: gx: 4 (over y, core), gz: 2 (over x), ta: 4 (over z).
Axes of the slice: x: 2, y: 2, z: 4, core: 2. Of those that a mesh axis runs over, the one named last changes fastest.
Arguments:
- links: float32 [4, 2, 3, 3, 16, 8, 512], P(None, None, None, None, 'ta', 'gz', 'gx'), may hold values from -1 to 1, as said below
Outputs:
- force: float32 [4, 2, 3, 3, 16, 8, 512], P(None, None, None, None, 'ta', 'gz', 'gx')
Inputs may be any that keep to these rules, and one draw needn't show every extreme that they name: Every link matrix (real part links[mu, 0], imaginary part links[mu, 1]) is special unitary, up to float32 rounding.
All inputs are finite; a program needn't handle non-finite values.
Results may differ from a plain program's by a relative error of at most 0.0003.
Values sent between devices are 32-bit elements; how exact they have to be, the bound alone decides.
A program may use at most 64 MiB of HBM per device.

v0:
```python
import jax
import jax.numpy as jnp
from jax import lax
from jax.sharding import PartitionSpec as P

NX = 16


COEFF = -1.9


def padded(block, sides, width):
    for axis, dim in sides:
        count = lax.axis_size(axis)
        forward = [(i, i + 1) for i in range(count - 1)]
        forward.append((count - 1, 0))
        backward = [(target, source) for source, target in forward]
        low = lax.ppermute(
            lax.slice_in_dim(block, block.shape[dim] - width, None, axis=dim), axis, forward
        )
        high = lax.ppermute(lax.slice_in_dim(block, 0, width, axis=dim), axis, backward)
        block = jnp.concatenate([low, block, high], axis=dim)
    return block


def matprod(left, right):
    total = left[:, 0][:, None] * right[0][None, :]
    total = total + left[:, 1][:, None] * right[1][None, :]
    return total + left[:, 2][:, None] * right[2][None, :]


def complex_mul(left, right):
    return (
        matprod(left[0], right[0]) - matprod(left[1], right[1]),
        matprod(left[0], right[1]) + matprod(left[1], right[0]),
    )


def dagger(matrix):
    return (jnp.swapaxes(matrix[0], 0, 1), -jnp.swapaxes(matrix[1], 0, 1))


def unit_step(direction, sign):
    offset = [0, 0, 0, 0]
    offset[direction] = sign
    return tuple(offset)


def joined(first_step, second_step):
    return tuple((first_step[position] + second_step[position] for position in range(4)))


def gauge_force(fetch_link):
    blocks = []
    still = (0, 0, 0, 0)
    for direction in range(4):
        ahead = unit_step(direction, 1)
        summed = None
        for transverse in range(4):
            if transverse == direction:
                continue
            side_up = unit_step(transverse, 1)
            side_down = unit_step(transverse, -1)
            upper = complex_mul(
                complex_mul(fetch_link(transverse, ahead), dagger(fetch_link(direction, side_up))),
                dagger(fetch_link(transverse, still)),
            )
            lower = complex_mul(
                complex_mul(
                    dagger(fetch_link(transverse, joined(ahead, side_down))),
                    dagger(fetch_link(direction, side_down)),
                ),
                fetch_link(transverse, side_down),
            )
            staple = (upper[0] + lower[0], upper[1] + lower[1])
            summed = staple if summed is None else (summed[0] + staple[0], summed[1] + staple[1])
        loop_matrix = complex_mul(fetch_link(direction, still), summed)
        real_part = 0.5 * (loop_matrix[0] - jnp.swapaxes(loop_matrix[0], 0, 1))
        imag_part = 0.5 * (loop_matrix[1] + jnp.swapaxes(loop_matrix[1], 0, 1))
        trace_third = (loop_matrix[1][0, 0] + loop_matrix[1][1, 1] + loop_matrix[1][2, 2]) / 3.0
        identity = jnp.eye(3, dtype=jnp.float32).reshape((3, 3) + (1,) * trace_third.ndim)
        imag_part = imag_part - identity * trace_third
        blocks.append(COEFF * jnp.stack([real_part, imag_part], axis=0))
    return jnp.stack(blocks, axis=0)


def complete_rows(wider):
    real0 = wider[:, 0, 0]
    imag0 = wider[:, 1, 0]
    real1 = wider[:, 0, 1]
    imag1 = wider[:, 1, 1]
    real_cols = []
    imag_cols = []
    for column in range(3):
        next_col = (column + 1) % 3
        last_col = (column + 2) % 3
        cross_real = (
            real0[:, next_col] * real1[:, last_col]
            - imag0[:, next_col] * imag1[:, last_col]
            - real0[:, last_col] * real1[:, next_col]
            + imag0[:, last_col] * imag1[:, next_col]
        )
        cross_imag = (
            real0[:, next_col] * imag1[:, last_col]
            + imag0[:, next_col] * real1[:, last_col]
            - real0[:, last_col] * imag1[:, next_col]
            - imag0[:, last_col] * real1[:, next_col]
        )
        real_cols.append(cross_real)
        imag_cols.append(-cross_imag)
    third = jnp.stack([jnp.stack(real_cols, axis=1), jnp.stack(imag_cols, axis=1)], axis=1)
    return jnp.concatenate([wider, third[:, :, None]], axis=2)


def per_device(links):
    payload = links[:, :, 0:2]
    wider = padded(payload, (("ta", 4), ("gz", 5)), 1)
    wider = padded(wider, (("gx", 6),), NX)
    wider = complete_rows(wider)
    time_len = links.shape[4]
    depth_len = links.shape[5]
    flat_len = links.shape[6]
    column = lax.broadcasted_iota(jnp.int32, (flat_len,), 0) % NX
    right_edge = column == NX - 1
    left_edge = column == 0

    def fetch_link(direction, offset):
        start = NX + offset[2] * NX
        field = wider[
            direction,
            :,
            :,
            :,
            1 + offset[0] : 1 + offset[0] + time_len,
            1 + offset[1] : 1 + offset[1] + depth_len,
            start : start + flat_len,
        ]
        if offset[3] == 1:
            field = jnp.where(
                right_edge, jnp.roll(field, NX - 1, axis=5), jnp.roll(field, -1, axis=5)
            )
        elif offset[3] == -1:
            field = jnp.where(
                left_edge, jnp.roll(field, 1 - NX, axis=5), jnp.roll(field, 1, axis=5)
            )
        return (field[0], field[1])

    return gauge_force(fetch_link)


def solution(mesh):
    return jax.shard_map(
        per_device,
        mesh=mesh,
        in_specs=(P(None, None, None, None, "ta", "gz", "gx"),),
        out_specs=P(None, None, None, None, "ta", "gz", "gx"),
        check_vma=False,
    )
```

profile of v0, /device:TPU:0, one launch (start us, length us, event | category | flops | bytes accessed | tf_op | source)
XLA Modules:
  0.0 74.1 jit_solution(11909638522552661117)
XLA Ops:
  0.0 1.0 %fusion.24 = (f32[4,2,2,3,1,4,128]{6,5,4,3,2,1,0:T(4,128)S(1)}, f32[4,2,2,3,1,4,128]{6,5,4,3,2,1,0:T(4,128)S(1)}) fusion(f32[4,2,3,3,4,4,128]{6,5,4,3,2,1,0:T(4,128)} %param.1), kind=kLoop, calls=%fused_computation.721 | loop fusion | bytes 393216 | tf_op jit(solution)/shard_map/slice | solution.py:21
  1.0 3.1 %collective-permute-start = (f32[4,2,2,3,1,4,128]{6,0,5,4,3,2,1:T(4,128)S(1)}, f32[4,2,2,3,1,4,128]{6,0,5,4,3,2,1:T(4,128)S(1)}, u32[]{:S(2)}, u32[]{:S(2)}) collective-permute-start(f32[4,2,2,3,1,4,128]{6,0,5,4,3,2,1:T(4,128)S(1)} %copy.19), channel_id=1, source_target_pairs={{0,1},{1,2},{2,3},{3,0},{4,5},{5,6},{6,7},{7,4},{8,9},{9,10},{10,1... | collective-permute-start | bytes 294920 | tf_op jit(solution)/shard_map/ppermute | solution.py:18
  4.2 2.1 %collective-permute-start.1 = (f32[4,2,2,3,1,4,128]{6,0,5,4,3,2,1:T(4,128)S(1)}, f32[4,2,2,3,1,4,128]{6,0,5,4,3,2,1:T(4,128)S(1)}, u32[]{:S(2)}, u32[]{:S(2)}) collective-permute-start(f32[4,2,2,3,1,4,128]{6,0,5,4,3,2,1:T(4,128)S(1)} %copy.21), channel_id=1, source_target_pairs={{1,0},{2,1},{3,2},{0,3},{5,4},{6,5},{7,6},{4,7},{9,8},{10,9},{11,1... | collective-permute-start | bytes 294920 | tf_op jit(solution)/shard_map/ppermute | solution.py:21
  6.3 1.0 %slice.3254 = f32[4,2,2,3,4,4,128]{6,5,4,3,2,1,0:T(4,128)S(1)} slice(f32[4,2,3,3,4,4,128]{6,5,4,3,2,1,0:T(4,128)} %param.1), slice={[0:4], [0:2], [0:2], [0:3], [0:4], [0:4], [0:128]} | slice | bytes 786432 | tf_op jit(solution)/shard_map/slice | solution.py:116
  7.3 2.2 %collective-permute-done = f32[4,2,2,3,1,4,128]{6,0,5,4,3,2,1:T(4,128)S(1)} collective-permute-done((f32[4,2,2,3,1,4,128]{6,0,5,4,3,2,1:T(4,128)S(1)}, f32[4,2,2,3,1,4,128]{6,0,5,4,3,2,1:T(4,128)S(1)}, u32[]{:S(2)}, u32[]{:S(2)}) %collective-permute-start) | collective-permute-done | bytes 98336 | tf_op jit(solution)/shard_map/ppermute | solution.py:18
  9.5 0.4 copy_dynamic-update-slice_fusion
  9.9 0.7 collective-permute-done.1
  10.7 1.6 %collective-permute-start.2 = (f32[4,2,2,3,6,1,128]{6,0,5,4,3,2,1:T(4,128)S(1)}, f32[4,2,2,3,6,1,128]{6,0,5,4,3,2,1:T(4,128)S(1)}, u32[]{:S(2)}, u32[]{:S(2)}) collective-permute-start(f32[4,2,2,3,6,1,128]{6,0,5,4,3,2,1:T(4,128)S(1)} %get-tuple-element.97), channel_id=1, source_target_pairs={{0,4},{4,0},{1,5},{5,1},{2,6},{6,2},{3,7},{7,3},{8,12},{12,8},{9,1... | collective-permute-start | bytes 442376 | tf_op jit(solution)/shard_map/ppermute | solution.py:18
  12.2 0.5 collective-permute-start.3
  12.8 4.6 %collective-permute-done.2 = f32[4,2,2,3,6,1,128]{6,0,5,4,3,2,1:T(4,128)S(1)} collective-permute-done((f32[4,2,2,3,6,1,128]{6,0,5,4,3,2,1:T(4,128)S(1)}, f32[4,2,2,3,6,1,128]{6,0,5,4,3,2,1:T(4,128)S(1)}, u32[]{:S(2)}, u32[]{:S(2)}) %collective-permute-start.2) | collective-permute-done | bytes 147488 | tf_op jit(solution)/shard_map/ppermute | solution.py:18
  17.4 1.7 %collective-permute-done.3 = f32[4,2,2,3,6,1,128]{6,0,5,4,3,2,1:T(4,128)S(1)} collective-permute-done((f32[4,2,2,3,6,1,128]{6,0,5,4,3,2,1:T(4,128)S(1)}, f32[4,2,2,3,6,1,128]{6,0,5,4,3,2,1:T(4,128)S(1)}, u32[]{:S(2)}, u32[]{:S(2)}) %collective-permute-start.3) | collective-permute-done | bytes 147488 | tf_op jit(solution)/shard_map/ppermute | solution.py:21
  19.2 0.2 pad_maximum_fusion.2
  19.4 0.5 fusion.22
  20.0 1.7 %collective-permute-start.5 = (f32[4,2,2,3,6,6,16]{6,0,5,4,3,2,1:T(4,128)S(1)}, f32[4,2,2,3,6,6,16]{6,0,5,4,3,2,1:T(4,128)S(1)}, u32[]{:S(2)}, u32[]{:S(2)}) collective-permute-start(f32[4,2,2,3,6,6,16]{6,0,5,4,3,2,1:T(4,128)S(1)} %get-tuple-element.92), channel_id=1, source_target_pairs={{8,0},{16,8},{24,16},{0,24},{9,1},{17,9},{25,17},{1,25},{10,2},{18... | collective-permute-start | bytes 331784 | tf_op jit(solution)/shard_map/ppermute | solution.py:21
  21.8 18.3 %collective-permute-done.4 = f32[4,2,2,3,6,6,16]{6,0,5,4,3,2,1:T(4,128)S(1)} collective-permute-done((f32[4,2,2,3,6,6,16]{6,0,5,4,3,2,1:T(4,128)S(1)}, f32[4,2,2,3,6,6,16]{6,0,5,4,3,2,1:T(4,128)S(1)}, u32[]{:S(2)}, u32[]{:S(2)}) %collective-permute-start.4) | collective-permute-done | bytes 110624 | tf_op jit(solution)/shard_map/ppermute | solution.py:18
  40.1 0.9 %collective-permute-done.5 = f32[4,2,2,3,6,6,16]{6,0,5,4,3,2,1:T(4,128)S(1)} collective-permute-done((f32[4,2,2,3,6,6,16]{6,0,5,4,3,2,1:T(4,128)S(1)}, f32[4,2,2,3,6,6,16]{6,0,5,4,3,2,1:T(4,128)S(1)}, u32[]{:S(2)}, u32[]{:S(2)}) %collective-permute-start.5) | collective-permute-done | bytes 110624 | tf_op jit(solution)/shard_map/ppermute | solution.py:21
  41.0 1.4 %pad_maximum_fusion.1 = f32[4,2,2,3,6,6,160]{6,0,5,4,3,2,1:T(4,128)S(1)} fusion(f32[4,2,2,3,6,6,16]{6,0,5,4,3,2,1:T(4,128)S(1)} %collective-permute-done.5, f32[4,2,2,3,6,1,128]{6,0,5,4,3,2,1:T(4,128)S(1)} %collective-permute-done.3, f32[4,2,2,3,6,4,128]{6,0,5,4,3,2,1:T(4,128)S(1)} %constant_dynamic-update-slice_fusion, ...), kind=kLoop, calls=%fused_computation.1 | loop fusion | flops 1105920 | bytes 2211840 | tf_op jit(solution)/shard_map/concatenate | solution.py:22
  42.4 0.3 slice_bitcast_fusion.2
  42.7 0.2 multiply_add_fusion.1
  42.9 0.2 multiply_add_fusion.2
  43.1 0.2 subtract_negate_fusion.2
  43.3 0.2 maximum_bitcast_fusion.1
  43.5 0.2 maximum_bitcast_fusion
  43.8 0.3 fusion.21
  44.0 2.5 %pad_maximum_fusion = f32[4,2,3,3,6,6,160]{6,0,5,4,3,2,1:T(4,128)S(1)} fusion(f32[4,2,1,3,6,6,160]{6,0,5,4,3,2,1:T(4,128)S(1)} %maximum_bitcast_fusion, f32[4,2,2,3,6,6,16]{6,0,5,4,3,2,1:T(4,128)S(1)} %collective-permute-done.5, f32[4,2,2,3,6,1,128]{6,0,5,4,3,2,1:T(4,128)S(1)} %collective-permute-done.3, ...), kind=kLoop, calls=%fused_computation | loop fusion | flops 2073600 | bytes 3317760 | tf_op jit(solution)/shard_map/concatenate | solution.py:112
  46.5 2.5 %slice_negate_fusion.23 = (f32[1,1,3,3,4,4,128]{6,0,5,4,3,2,1:T(1,128)S(1)}, f32[1,1,3,3,4,4,128]{6,0,5,4,3,2,1:T(1,128)S(1)}, f32[1,1,3,3,4,4,128]{6,0,5,4,3,2,...) fusion(f32[4,2,3,3,6,6,160]{6,0,5,4,3,2,1:T(4,128)S(1)} %pad_ma, ...), kind=kLoop, calls=%fused_computation.80 | loop fusion | flops 55296 | bytes 2654208 | tf_op jit(solution)/shard_map/neg | solution.py:40
  49.3 2.7 %fusion.18 = (f32[1,1,3,3,4,4,128]{6,0,5,4,3,2,1:T(1,128)S(1)}, f32[1,1,3,3,4,4,128]{6,0,5,4,3,2,1:T(1,128)S(1)}, f32[1,1,3,3,4,4,128]{6,0,5,4,3,2,1:T(1,128)S(1...) fusion(f32[4,2,3,3,6,6,160]{6,0,5,4,3,2,1:T(4,128)S(1)} %pad_ma, ...), kind=kLoop, calls=%fused_computation.715 | loop fusion | flops 147456 | bytes 2801664 | tf_op jit(solution)/shard_map/slice | solution.py:146
  52.1 2.5 %fusion.19 = (f32[1,1,3,3,4,4,128]{6,0,5,4,3,2,1:T(1,128)S(1)}, f32[1,1,3,3,4,4,128]{6,0,5,4,3,2,1:T(1,128)S(1)}, f32[1,1,3,3,4,4,128]{6,0,5,4,3,2,1:T(1,128)S(1...) fusion(f32[4,2,3,3,6,6,160]{6,0,5,4,3,2,1:T(4,128)S(1)} %pad_ma, ...), kind=kLoop, calls=%fused_computation.716 | loop fusion | flops 73728 | bytes 2801664 | tf_op jit(solution)/shard_map/slice | solution.py:146
  54.6 2.9 %fusion.20 = (f32[1,2,3,3,4,4,128]{6,0,5,4,3,2,1:T(1,128)S(1)}, f32[1,2,3,3,4,4,128]{6,0,5,4,3,2,1:T(1,128)S(1)}, f32[1,2,3,3,4,4,128]{6,0,5,4,3,2,1:T(1,128)S(1...) fusion(f32[4,2,3,3,6,6,160]{6,0,5,4,3,2,1:T(4,128)S(1)} %pad_ma, ...), kind=kLoop, calls=%fused_computation.717 | loop fusion | bytes 2949120 | tf_op jit(solution)/shard_map/slice | solution.py:129
  57.8 0.1 slice.4522
  58.1 0.1 slice.4124
  58.2 0.1 slice.4460
  58.4 0.1 slice.4458
  58.8 0.4 slice.4152
  59.9 0.1 fusion.35
  60.1 0.1 fusion.34
  60.2 0.1 fusion.37
  60.4 0.1 fusion.36
  60.5 0.1 fusion.31
  60.7 0.1 fusion.30
  60.8 0.1 fusion.33
  61.0 0.1 fusion.32
  61.1 0.1 fusion.27
  61.3 0.1 fusion.26
  61.4 0.1 fusion.29
  61.6 0.1 fusion.28
  61.7 0.7 maximum_select_fusion
  64.9 0.4 maximum_select_fusion.11
  65.6 0.5 maximum_select_fusion.6
  66.4 0.7 maximum_select_fusion.1
  68.0 0.3 pad_maximum_fusion.9
  68.3 0.4 add_add_fusion.2
  68.8 0.4 add_add_fusion.1
  69.3 0.4 add_add_fusion.10
  69.7 0.4 add_add_fusion.11
  70.2 0.2 multiply_bitcast_fusion
  70.3 0.2 multiply_bitcast_fusion.1
  70.7 0.4 add_add_fusion.29
  71.1 0.4 add_add_fusion.28
  71.5 0.2 multiply_bitcast_fusion.3
  71.8 0.4 add_add_fusion.20
  72.2 0.4 add_add_fusion.19
  72.7 0.2 multiply_bitcast_fusion.2
  73.1 0.9 %pad_maximum_fusion.3 = f32[4,2,3,3,4,4,128]{6,5,4,3,2,1,0:T(4,128)} fusion(f32[1,2,3,3,4,4,128]{6,5,4,3,2,1,0:T(4,128)S(1)} %maximum_multiply_fusion.3, f32[1,2,3,3,4,4,128]{6,5,4,3,2,1,0:T(4,128)S(1)} %maximum_multiply_fusion.2, f32[1,2,3,3,4,4,128]{6,5,4,3,2,1,0:T(4,128)S(1)} %maximum_multiply_fusion.1, ...), kind=kLoop, calls=%fused_computation.4 | loop fusion | flops 442368 | bytes 1179648 | tf_op jit(solution)/shard_map/stack | solution.py:84
  (253 shorter events, 5.4 us)
Async XLA Ops:
  1.0 8.5 %collective-permute-start = (f32[4,2,2,3,1,4,128]{6,0,5,4,3,2,1:T(4,128)S(1)}, f32[4,2,2,3,1,4,128]{6,0,5,4,3,2,1:T(4,128)S(1)}, u32[]{:S(2)}, u32[]{:S(2)}) collective-permute-start(f32[4,2,2,3,1,4,128]{6,0,5,4,3,2,1:T(4,128)S(1)} %copy.19), channel_id=1, source_target_pairs={{0,1},{1,2},{2,3},{3,0},{4,5},{5,6},{6,7},{7,4},{8,9},{9,10},{10,1... | collective-permute-start | bytes 294920 | tf_op jit(solution)/shard_map/ppermute | solution.py:18
  4.2 6.4 %collective-permute-start.1 = (f32[4,2,2,3,1,4,128]{6,0,5,4,3,2,1:T(4,128)S(1)}, f32[4,2,2,3,1,4,128]{6,0,5,4,3,2,1:T(4,128)S(1)}, u32[]{:S(2)}, u32[]{:S(2)}) collective-permute-start(f32[4,2,2,3,1,4,128]{6,0,5,4,3,2,1:T(4,128)S(1)} %copy.21), channel_id=1, source_target_pairs={{1,0},{2,1},{3,2},{0,3},{5,4},{6,5},{7,6},{4,7},{9,8},{10,9},{11,1... | collective-permute-start | bytes 294920 | tf_op jit(solution)/shard_map/ppermute | solution.py:21
  10.7 6.8 %collective-permute-start.2 = (f32[4,2,2,3,6,1,128]{6,0,5,4,3,2,1:T(4,128)S(1)}, f32[4,2,2,3,6,1,128]{6,0,5,4,3,2,1:T(4,128)S(1)}, u32[]{:S(2)}, u32[]{:S(2)}) collective-permute-start(f32[4,2,2,3,6,1,128]{6,0,5,4,3,2,1:T(4,128)S(1)} %get-tuple-element.97), channel_id=1, source_target_pairs={{0,4},{4,0},{1,5},{5,1},{2,6},{6,2},{3,7},{7,3},{8,12},{12,8},{9,1... | collective-permute-start | bytes 442376 | tf_op jit(solution)/shard_map/ppermute | solution.py:18
  12.2 7.0 %collective-permute-start.3 = (f32[4,2,2,3,6,1,128]{6,0,5,4,3,2,1:T(4,128)S(1)}, f32[4,2,2,3,6,1,128]{6,0,5,4,3,2,1:T(4,128)S(1)}, u32[]{:S(2)}, u32[]{:S(2)}) collective-permute-start(f32[4,2,2,3,6,1,128]{6,0,5,4,3,2,1:T(4,128)S(1)} %get-tuple-element.98), channel_id=1, source_target_pairs={{4,0},{0,4},{5,1},{1,5},{6,2},{2,6},{7,3},{3,7},{12,8},{8,12},{13,... | collective-permute-start | bytes 442376 | tf_op jit(solution)/shard_map/ppermute | solution.py:21
  19.9 20.2 %collective-permute-start.4 = (f32[4,2,2,3,6,6,16]{6,0,5,4,3,2,1:T(4,128)S(1)}, f32[4,2,2,3,6,6,16]{6,0,5,4,3,2,1:T(4,128)S(1)}, u32[]{:S(2)}, u32[]{:S(2)}) collective-permute-start(f32[4,2,2,3,6,6,16]{6,0,5,4,3,2,1:T(4,128)S(1)} %get-tuple-element.91), channel_id=1, source_target_pairs={{0,8},{8,16},{16,24},{24,0},{1,9},{9,17},{17,25},{25,1},{2,10},{10... | collective-permute-start | bytes 331784 | tf_op jit(solution)/shard_map/ppermute | solution.py:18
  20.0 21.0 %collective-permute-start.5 = (f32[4,2,2,3,6,6,16]{6,0,5,4,3,2,1:T(4,128)S(1)}, f32[4,2,2,3,6,6,16]{6,0,5,4,3,2,1:T(4,128)S(1)}, u32[]{:S(2)}, u32[]{:S(2)}) collective-permute-start(f32[4,2,2,3,6,6,16]{6,0,5,4,3,2,1:T(4,128)S(1)} %get-tuple-element.92), channel_id=1, source_target_pairs={{8,0},{16,8},{24,16},{0,24},{9,1},{17,9},{25,17},{1,25},{10,2},{18... | collective-permute-start | bytes 331784 | tf_op jit(solution)/shard_map/ppermute | solution.py:21
where the time goes:
time: 74.5 us; the launch traced here: 74.1 us
  waiting for transfers between devices  28.4 us (38%)
  other arithmetic  22.7 us (30%)
  local copies, waits for them, and re-layouts  11.9 us (16%)
  starting transfers between devices  9.08 us (12%)
  between operations  2.08 us (3%)
    ppermute x3, waiting for transfers between devices, padded(): lax.ppermute(lax.slice_in_dim(block, block.shape[dim] - width, None, axis...  25.1 us
    slice x2, other arithmetic, fetch_link(): return (field[0], field[1])  5.21 us
    ppermute x3, starting transfers between devices, padded(): lax.ppermute(lax.slice_in_dim(block, block.shape[dim] - width, None, axis...  4.72 us
    ppermute x3, starting transfers between devices, padded(): lax.ppermute(lax.slice_in_dim(block, 0, width, axis=dim), axis, backward)  4.36 us
    ppermute x3, waiting for transfers between devices, padded(): lax.ppermute(lax.slice_in_dim(block, 0, width, axis=dim), axis, backward)  3.28 us
    slice x1, local copies, waits for them, and re-layouts, fetch_link(): wider[direction, :, :, :, 1 + offset[0]:1 + offset[0] + time_len, 1 + off...  2.89 us
    neg x17, other arithmetic, dagger(): return (jnp.swapaxes(matrix[0], 0, 1), -jnp.swapaxes(matrix[1], 0, 1))  2.77 us
    concatenate x1, other arithmetic, complete_rows(): return jnp.concatenate([wider, third[:, :, None]], axis=2)  2.48 us
  transfers between devices with their start and end apart: 6, of which 6 were waited for; matrix products, arithmetic and copies ran while one was open for 2% of the time, Pallas kernels for 0%

commit v1 on v0

v1 whole, which is shorter than its diff:
```python
import functools

import jax
import jax.numpy as jnp
from jax import lax
from jax.experimental import pallas as pl
from jax.experimental.pallas import tpu as pltpu
from jax.sharding import PartitionSpec as P

NX = 16
COEFF = -1.9
AXES = ("ta", "gz", "gx")
SUB, LANES = 8, 128


def others(d):
    return [m for m in range(4) if m != d]


class Lattice:
    def __init__(self, depth):
        self.depth = depth
        self.per = SUB // depth
        self.ygroups = LANES // NX
        self.row = lax.broadcasted_iota(jnp.int32, (SUB, LANES), 0)
        self.lane = lax.broadcasted_iota(jnp.int32, (SUB, LANES), 1)
        self.zrow = self.row % depth
        self.xcol = self.lane % NX

    def rows(self, value, shift):
        shift %= SUB
        return pltpu.roll(value, shift, 0) if shift else value

    def lanes(self, value, shift):
        shift %= LANES
        return pltpu.roll(value, shift, 1) if shift else value


def entry(left, right, i, j, part, left_h, right_h):
    total = None
    for k in range(3):
        li = (k, i) if left_h else (i, k)
        ri = (j, k) if right_h else (k, j)
        lr, lm = left[0][li[0]][li[1]], left[1][li[0]][li[1]]
        rr, rm = right[0][ri[0]][ri[1]], right[1][ri[0]][ri[1]]
        if part == 0:
            first, second = lr * rr, lm * rm
            minus = left_h == right_h
        elif left_h:
            first, second = lr * rm, lm * rr
            minus = True
        else:
            first, second = lm * rr, lr * rm
            minus = right_h
        value = first - second if minus else first + second
        total = value if total is None else total + value
    return total


def product(left, right, left_h=False, right_h=False):
    return [
        [[entry(left, right, i, j, part, left_h, right_h) for j in range(3)] for i in range(3)]
        for part in range(2)
    ]


def projected(left, right, left_h=False, right_h=False):
    get = lambda i, j, part: entry(left, right, i, j, part, left_h, right_h)
    pairs = ((0, 1), (0, 2), (1, 2))
    real = [get(i, j, 0) - get(j, i, 0) for i, j in pairs]
    imag = [get(i, j, 1) + get(j, i, 1) for i, j in pairs]
    diag = [get(i, i, 1) for i in range(3)]
    third = (diag[0] + diag[1] + diag[2]) * (1.0 / 3.0)
    return real + imag + [diag[0] - third, diag[1] - third]


def third_row(real, imag):
    rows_r, rows_i = [], []
    for column in range(3):
        n, l = (column + 1) % 3, (column + 2) % 3
        rows_r.append(
            real[0][n] * real[1][l]
            - imag[0][n] * imag[1][l]
            - real[0][l] * real[1][n]
            + imag[0][l] * imag[1][n]
        )
        rows_i.append(
            real[0][l] * imag[1][n]
            + imag[0][l] * real[1][n]
            - real[0][n] * imag[1][l]
            - imag[0][n] * real[1][l]
        )
    return rows_r, rows_i


def sizes(depth, halves):
    yg = LANES // NX
    per = SUB // depth

    def rows(count):
        return (
            -(-count // per) * SUB,
            -(-count // depth) * SUB * halves,
            -(-count // yg) * SUB * halves,
        )

    return rows(36), rows(24)


def kernel(
    counts, depth, halves, u, out,
    st, sz, sy, rt, rz, ry, qt, qz, qy, pt, pz, py, acc, send, recv,
):
    g = Lattice(depth)
    me = [lax.axis_index(a) for a in AXES]
    nxt = [lax.rem(me[i] + 1, counts[i]) for i in range(3)]
    prv = [lax.rem(me[i] + counts[i] - 1, counts[i]) for i in range(3)]

    def device(i, index):
        where = list(me)
        where[i] = index
        by = dict(zip(AXES, where))
        return (by["gx"], by["gz"], by["ta"])

    barrier = pltpu.get_barrier_semaphore()
    for i in range(3):
        for index in (nxt[i], prv[i]):
            pl.semaphore_signal(
                barrier, inc=1, device_id=device(i, index), device_id_type=pl.DeviceIdType.MESH
            )

    def load(m, part, i, j, h):
        return u[m, part, i, j, h * SUB : (h + 1) * SUB, :]

    def comps(d):
        return [(m, part, i, j) for m in others(d) for part in range(2) for i in range(2) for j in range(3)]

    cs = comps(0)
    for c0 in range(0, len(cs), g.per):
        value = None
        for k in range(g.per):
            x = g.rows(load(*cs[c0 + k], 0), depth * k)
            value = x if value is None else jnp.where(g.row >= depth * k, x, value)
        st[c0 // g.per * SUB : (c0 // g.per + 1) * SUB, :] = value
    cs = comps(1)
    for c0 in range(0, len(cs), depth):
        for h in range(halves):
            value = None
            for k in range(depth):
                x = g.rows(load(*cs[c0 + k], h), k)
                value = x if value is None else jnp.where(g.zrow >= k, x, value)
            r = (c0 // depth * halves + h) * SUB
            sz[r : r + SUB, :] = value
    cs = comps(2)
    for c0 in range(0, len(cs), g.ygroups):
        for h in range(halves):
            value = None
            for k in range(min(g.ygroups, len(cs) - c0)):
                x = g.lanes(load(*cs[c0 + k], h), NX * k)
                value = x if value is None else jnp.where(g.lane >= NX * k, x, value)
            r = (c0 // g.ygroups * halves + h) * SUB
            sy[r : r + SUB, :] = value

    pl.semaphore_wait(barrier, 6)

    def remote(src, dst, slot, i, index):
        return pltpu.make_async_remote_copy(
            src_ref=src, dst_ref=dst, send_sem=send.at[slot], recv_sem=recv.at[slot],
            device_id=device(i, index), device_id_type=pl.DeviceIdType.MESH,
        )

    first = [
        remote(st, rt, 0, 0, prv[0]),
        remote(sz, rz, 1, 1, prv[1]),
        remote(sy, ry, 2, 2, prv[2]),
    ]
    second = [
        remote(qt, pt, 3, 0, nxt[0]),
        remote(qz, pz, 4, 1, nxt[1]),
        remote(qy, py, 5, 2, nxt[2]),
    ]
    for copy in first:
        copy.start()

    def matrix(m, h):
        return [[[load(m, part, i, j, h) for j in range(3)] for i in range(3)] for part in range(2)]

    def ahead(m, d, h):
        index = {c: n for n, c in enumerate(comps(d))} if d < 3 else None

        def get(part, i, j):
            v = load(m, part, i, j, h)
            if d == 3:
                return jnp.where(g.xcol == NX - 1, g.lanes(v, NX - 1), g.lanes(v, -1))
            c = index[(m, part, i, j)]
            if d == 0:
                if h + 1 < halves:
                    beyond = g.rows(load(m, part, i, j, h + 1), -depth)
                else:
                    r = c // g.per * SUB
                    beyond = g.rows(rt[r : r + SUB, :], SUB - depth - depth * (c % g.per))
                return jnp.where(g.row >= SUB - depth, beyond, g.rows(v, -depth))
            if d == 1:
                r = (c // depth * halves + h) * SUB
                edge = g.rows(rz[r : r + SUB, :], depth - 1 - c % depth)
                return jnp.where(g.zrow == depth - 1, edge, g.rows(v, -1))
            r = (c // g.ygroups * halves + h) * SUB
            edge = g.lanes(ry[r : r + SUB, :], LANES - NX - NX * (c % g.ygroups))
            return jnp.where(g.lane >= LANES - NX, edge, g.lanes(v, -NX))

        known = 3 if d == 3 else 2
        real = [[get(0, i, j) for j in range(3)] for i in range(known)]
        imag = [[get(1, i, j) for j in range(3)] for i in range(known)]
        if known == 2:
            third_r, third_i = third_row(real, imag)
            real.append(third_r)
            imag.append(third_i)
        return [real, imag]

    seen = set()

    def add(m, c, h, value):
        r = ((m * 8 + c) * halves + h) * SUB
        if (m, c, h) in seen:
            acc[r : r + SUB, :] += value
        else:
            seen.add((m, c, h))
            acc[r : r + SUB, :] = value

    def lower(m, d, h, q):
        base = others(d).index(m) * 8
        if d == 3:
            for c in range(8):
                add(m, c, h, jnp.where(g.xcol == 0, g.lanes(q[c], 1 - NX), g.lanes(q[c], 1)))
        elif d == 2:
            for c in range(8):
                add(m, c, h, jnp.where(g.lane >= NX, g.lanes(q[c], NX), 0.0))
            for c0 in range(0, 8, g.ygroups):
                value = None
                for k in range(g.ygroups):
                    x = g.lanes(q[c0 + k], NX * (k + 1))
                    value = x if value is None else jnp.where(g.lane >= NX * k, x, value)
                r = ((base + c0) // g.ygroups * halves + h) * SUB
                qy[r : r + SUB, :] = value
        elif d == 1:
            for c in range(8):
                add(m, c, h, jnp.where(g.zrow > 0, g.rows(q[c], 1), 0.0))
            for c0 in range(0, 8, depth):
                value = None
                for k in range(depth):
                    x = g.rows(q[c0 + k], k + 1 - depth)
                    value = x if value is None else jnp.where(g.zrow >= k, x, value)
                r = ((base + c0) // depth * halves + h) * SUB
                qz[r : r + SUB, :] = value
        else:
            for c in range(8):
                moved = g.rows(q[c], depth)
                add(m, c, h, jnp.where(g.row >= depth, moved, 0.0))
                if h + 1 < halves:
                    add(m, c, h + 1, jnp.where(g.row < depth, moved, 0.0))
            if h + 1 == halves:
                for c0 in range(0, 8, g.per):
                    value = None
                    for k in range(g.per):
                        x = g.rows(q[c0 + k], depth * (k + 1))
                        value = x if value is None else jnp.where(g.row >= depth * k, x, value)
                    r = (base + c0) // g.per * SUB
                    qt[r : r + SUB, :] = value

    def plane(mu, nu, h):
        here_mu, here_nu = matrix(mu, h), matrix(nu, h)
        a = product(ahead(nu, mu, h), ahead(mu, nu, h), right_h=True)
        e = product(here_mu, a)
        upper = projected(e, here_nu, right_h=True)
        for c in range(8):
            add(mu, c, h, upper[c])
            add(nu, c, h, -upper[c])
        lower(mu, nu, h, projected(e, here_nu, left_h=True))
        c_matrix = product(a, here_nu, right_h=True)
        lower(nu, mu, h, projected(c_matrix, here_mu))

    waits = {(0, 3): [0], (0, 1): [1], (0, 2): [2]}
    starts = {(0, 2): [0], (1, 2): [1], (2, 3): [2]}
    for pair in ((0, 3), (0, 1), (0, 2), (1, 3), (1, 2), (2, 3)):
        for h in range(halves):
            if h == (halves - 1 if pair == (0, 3) else 0):
                for i in waits.get(pair, ()):
                    first[i].wait_recv()
            plane(pair[0], pair[1], h)
        for i in starts.get(pair, ()):
            second[i].start()

    for copy in second:
        copy.wait_recv()
    for m in range(4):
        for h in range(halves):
            f = []
            for c in range(8):
                r = ((m * 8 + c) * halves + h) * SUB
                value = acc[r : r + SUB, :]
                for d in others(m):
                    b = others(d).index(m) * 8 + c
                    if d == 0 and h == 0:
                        r = b // g.per * SUB
                        x = g.rows(pt[r : r + SUB, :], -depth * (b % g.per))
                        value = value + jnp.where(g.row < depth, x, 0.0)
                    elif d == 1:
                        r = (b // depth * halves + h) * SUB
                        x = g.rows(pz[r : r + SUB, :], -(b % depth))
                        value = value + jnp.where(g.zrow == 0, x, 0.0)
                    elif d == 2:
                        r = (b // g.ygroups * halves + h) * SUB
                        x = g.lanes(py[r : r + SUB, :], -NX * (b % g.ygroups))
                        value = value + jnp.where(g.lane < NX, x, 0.0)
                f.append(value * (COEFF * 0.5 if c < 6 else COEFF))

            def put(part, i, j, value):
                out[m, part, i, j, h * SUB : (h + 1) * SUB, :] = value

            for n, (i, j) in enumerate(((0, 1), (0, 2), (1, 2))):
                put(0, i, j, f[n])
                put(0, j, i, -f[n])
                put(1, i, j, f[3 + n])
                put(1, j, i, f[3 + n])
            for i in range(3):
                put(0, i, i, jnp.zeros((SUB, LANES), jnp.float32))
            put(1, 0, 0, f[6])
            put(1, 1, 1, f[7])
            put(1, 2, 2, -(f[6] + f[7]))
    for copy in first + second:
        copy.wait_send()


def per_device(counts, links):
    time_len, depth, flat = links.shape[4:]
    sites = time_len * depth
    assert flat == LANES and SUB % depth == 0 and sites % SUB == 0
    halves = sites // SUB
    rows1, rows2 = sizes(depth, halves)
    vmem = lambda r: pltpu.VMEM((r, LANES), jnp.float32)
    shape = links.shape[:4] + (sites, flat)
    out = pl.pallas_call(
        functools.partial(kernel, counts, depth, halves),
        out_shape=jax.ShapeDtypeStruct(shape, jnp.float32),
        in_specs=[pl.BlockSpec(memory_space=pltpu.VMEM)],
        out_specs=pl.BlockSpec(memory_space=pltpu.VMEM),
        scratch_shapes=[vmem(r) for r in rows1 + rows1 + rows2 + rows2]
        + [
            vmem(32 * sites),
            pltpu.SemaphoreType.DMA((6,)),
            pltpu.SemaphoreType.DMA((6,)),
        ],
        compiler_params=pltpu.CompilerParams(collective_id=0, has_side_effects=True),
        name="force",
    )(links.reshape(shape))
    return out.reshape(links.shape)


def solution(mesh):
    assert mesh.axis_names == ("gx", "gz", "ta")
    counts = tuple(mesh.shape[a] for a in AXES)
    spec = P(None, None, None, None, "ta", "gz", "gx")
    return jax.shard_map(
        functools.partial(per_device, counts),
        mesh=mesh,
        in_specs=(spec,),
        out_specs=spec,
        check_vma=False,
    )
```

time: 74.5 us -> 18.5 us (0.25)
  waiting for transfers between devices: 28.4 us -> 0 us
  other arithmetic: 22.7 us -> 0 us
  Pallas kernels: 0 us -> 16.4 us
  local copies, waits for them, and re-layouts: 11.9 us -> 1.92 us
  starting transfers between devices: 9.08 us -> 0 us
  between operations: 2.08 us -> 0.01 us
    ppermute x6 -> x0, waiting for transfers between devices: 28.4 us -> none  [the longest x3 25.1 us: padded(): lax.ppermute(lax.slice_in_dim(block, block.shape[dim] - width, None, axis...]
    pallas_call x0 -> x1, Pallas kernels: none -> 16.4 us  [per_device(): pl.pallas_call(functools.partial(kernel, counts, depth, halves), out_shap...]
    slice x33 -> x0, local copies, waits for them, and re-layouts: 9.72 us -> none  [the longest x1 2.89 us: fetch_link(): wider[direction, :, :, :, 1 + offset[0]:1 + offset[0] + time_len, 1 + off...]
    ppermute x6 -> x0, starting transfers between devices: 9.08 us -> none  [the longest x3 4.72 us: padded(): lax.ppermute(lax.slice_in_dim(block, block.shape[dim] - width, None, axis...]
    slice x4 -> x0, other arithmetic: 5.59 us -> none  [the longest x2 5.21 us: fetch_link(): return (field[0], field[1])]
    concatenate x3 -> x0, other arithmetic: 4.11 us -> none  [the longest x1 2.48 us: complete_rows(): return jnp.concatenate([wider, third[:, :, None]], axis=2)]
    add x14 -> x0, other arithmetic: 3.68 us -> none  [the longest x4 1.58 us: gauge_force(): summed[1] + staple[1]]
    neg x18 -> x0, other arithmetic: 2.99 us -> none  [the longest x17 2.77 us: dagger(): return (jnp.swapaxes(matrix[0], 0, 1), -jnp.swapaxes(matrix[1], 0, 1))]
  transfers between devices with their start and end apart: 6 -> 0, of which waited for: 6 -> 0; matrix products, arithmetic and copies ran while one was open for 2% -> 0% of each run, Pallas kernels for 0% -> 0%
where the time goes in v1:
time: 18.5 us; the launch traced here: 18.3 us
  Pallas kernels  16.4 us (89%)
  local copies, waits for them, and re-layouts  1.92 us (10%)
    pallas_call x1, Pallas kernels, per_device(): pl.pallas_call(functools.partial(kernel, counts, depth, halves), out_shap...  16.4 us
    unnamed x1, local copies, waits for them, and re-layouts  1.92 us

profile of v1, /device:TPU:0, one launch (start us, length us, event | category | flops | bytes accessed | tf_op | source)
XLA Modules:
  0.0 18.3 jit_solution(1949043499806832609)
XLA Ops:
  0.0 16.4 %force.1 = f32[4,2,3,3,16,128]{5,4,3,2,1,0:T(8,128)} custom-call(f32[4,2,3,3,16,128]{5,4,3,2,1,0:T(8,128)} %bitcast.3), custom_call_target="tpu_custom_call" | custom-call | tf_op jit(solution)/shard_map/force/pallas_call | solution.py:342
  16.4 1.9 %copy.3 = f32[4,2,3,3,4,4,128]{6,5,4,3,2,1,0:T(4,128)} copy(f32[4,2,3,3,4,4,128]{6,5,4,3,2,1,0:T(4,128)} %bitcast.2) | data formatting | bytes 1179648

commit v2 on v1

v2 whole, which is shorter than its diff:
```python
import functools

import jax
import jax.numpy as jnp
from jax import lax
from jax.experimental import pallas as pl
from jax.experimental.pallas import tpu as pltpu
from jax.sharding import PartitionSpec as P

NX = 16
COEFF = -1.9
AXES = ("ta", "gz", "gx")
SUB, LANES = 8, 128


def others(d):
    return [m for m in range(4) if m != d]


class Lattice:
    def __init__(self, depth):
        self.depth = depth
        self.per = SUB // depth
        self.ygroups = LANES // NX
        self.row = lax.broadcasted_iota(jnp.int32, (SUB, LANES), 0)
        self.lane = lax.broadcasted_iota(jnp.int32, (SUB, LANES), 1)
        self.zrow = self.row % depth
        self.xcol = self.lane % NX

    def rows(self, value, shift):
        shift %= SUB
        return pltpu.roll(value, shift, 0) if shift else value

    def lanes(self, value, shift):
        shift %= LANES
        return pltpu.roll(value, shift, 1) if shift else value


def entry(left, right, i, j, part, left_h, right_h):
    total = None
    for k in range(3):
        li = (k, i) if left_h else (i, k)
        ri = (j, k) if right_h else (k, j)
        lr, lm = left[0][li[0]][li[1]], left[1][li[0]][li[1]]
        rr, rm = right[0][ri[0]][ri[1]], right[1][ri[0]][ri[1]]
        if part == 0:
            first, second = lr * rr, lm * rm
            minus = left_h == right_h
        elif left_h:
            first, second = lr * rm, lm * rr
            minus = True
        else:
            first, second = lm * rr, lr * rm
            minus = right_h
        value = first - second if minus else first + second
        total = value if total is None else total + value
    return total


def product(left, right, left_h=False, right_h=False):
    return [
        [[entry(left, right, i, j, part, left_h, right_h) for j in range(3)] for i in range(3)]
        for part in range(2)
    ]


def projected(left, right, left_h=False, right_h=False):
    get = lambda i, j, part: entry(left, right, i, j, part, left_h, right_h)
    pairs = ((0, 1), (0, 2), (1, 2))
    real = [get(i, j, 0) - get(j, i, 0) for i, j in pairs]
    imag = [get(i, j, 1) + get(j, i, 1) for i, j in pairs]
    diag = [get(i, i, 1) for i in range(3)]
    third = (diag[0] + diag[1] + diag[2]) * (1.0 / 3.0)
    return real + imag + [diag[0] - third, diag[1] - third]


def third_row(real, imag):
    rows_r, rows_i = [], []
    for column in range(3):
        n, l = (column + 1) % 3, (column + 2) % 3
        rows_r.append(
            real[0][n] * real[1][l]
            - imag[0][n] * imag[1][l]
            - real[0][l] * real[1][n]
            + imag[0][l] * imag[1][n]
        )
        rows_i.append(
            real[0][l] * imag[1][n]
            + imag[0][l] * real[1][n]
            - real[0][n] * imag[1][l]
            - imag[0][n] * real[1][l]
        )
    return rows_r, rows_i


def sizes(depth, halves):
    yg = LANES // NX
    per = SUB // depth

    def rows(count):
        return (
            -(-count // per) * SUB,
            -(-count // depth) * SUB * halves,
            -(-count // yg) * SUB * halves,
        )

    return rows(36), rows(24)


PLANES = ((0, 3), (1, 3), (0, 2), (1, 2), (0, 1), (2, 3))


def force_terms(
    counts, depth, halves, hbm, acc,
    u, ahead_s, local_s, plaq_s, st, sz, sy, rt, rz, ry, qt, qz, qy, pt, pz, py,
    load_sem, send, recv,
):
    g = Lattice(depth)
    me = [lax.axis_index(a) for a in AXES]
    nxt = [lax.rem(me[i] + 1, counts[i]) for i in range(3)]
    prv = [lax.rem(me[i] + counts[i] - 1, counts[i]) for i in range(3)]

    def device(i, index):
        where = list(me)
        where[i] = index
        by = dict(zip(AXES, where))
        return (by["gx"], by["gz"], by["ta"])

    barrier = pltpu.get_barrier_semaphore()
    for i in range(3):
        for index in (nxt[i], prv[i]):
            pl.semaphore_signal(
                barrier, inc=1, device_id=device(i, index), device_id_type=pl.DeviceIdType.MESH
            )

    loads = {
        m: pltpu.make_async_copy(hbm.at[m, :, 0:2], u.at[m, :, 0:2], load_sem.at[m])
        for m in range(4)
    }
    last_rows = pltpu.make_async_copy(hbm.at[:, :, 2], u.at[:, :, 2], load_sem.at[4])
    for m in (3, 2, 1, 0):
        loads[m].start()
    last_rows.start()

    def load(m, part, i, j, h):
        return u[m, part, i, j, h * SUB : (h + 1) * SUB, :]

    def comps(d, m):
        return [(m, part, i, j) for part in range(2) for i in range(2) for j in range(3)]

    def all_comps(d):
        return [c for m in others(d) for c in comps(d, m)]

    def pack_t(m):
        cs, base = comps(0, m), 12 * others(0).index(m)
        for c0 in range(0, 12, g.per):
            value = None
            for k in range(g.per):
                x = g.rows(load(*cs[c0 + k], 0), depth * k)
                value = x if value is None else jnp.where(g.row >= depth * k, x, value)
            r = (base + c0) // g.per * SUB
            st[r : r + SUB, :] = value

    def pack_z(m):
        cs, base = comps(1, m), 12 * others(1).index(m)
        for c0 in range(0, 12, depth):
            for h in range(halves):
                value = None
                for k in range(depth):
                    x = g.rows(load(*cs[c0 + k], h), k)
                    value = x if value is None else jnp.where(g.zrow >= k, x, value)
                r = ((base + c0) // depth * halves + h) * SUB
                sz[r : r + SUB, :] = value

    def pack_y():
        cs = all_comps(2)
        for c0 in range(0, len(cs), g.ygroups):
            for h in range(halves):
                value = None
                for k in range(min(g.ygroups, len(cs) - c0)):
                    x = g.lanes(load(*cs[c0 + k], h), NX * k)
                    value = x if value is None else jnp.where(g.lane >= NX * k, x, value)
                r = (c0 // g.ygroups * halves + h) * SUB
                sy[r : r + SUB, :] = value

    for m in (3, 2, 1, 0):
        loads[m].wait()
        if m != 0:
            pack_t(m)
        if m != 1:
            pack_z(m)
    pack_y()

    def remote(src, dst, slot, i, index):
        return pltpu.make_async_remote_copy(
            src_ref=src, dst_ref=dst, send_sem=send.at[slot], recv_sem=recv.at[slot],
            device_id=device(i, index), device_id_type=pl.DeviceIdType.MESH,
        )

    def chunk(ref, d, m):
        n = ref.shape[0] // 3
        k = others(d).index(m)
        return ref.at[k * n : (k + 1) * n]

    first, second = {}, {}
    slot = 0
    for d, m in ((0, 3), (1, 3), (2, None), (0, 2), (1, 2), (0, 1), (1, 0)):
        src, dst = ((st, rt), (sz, rz), (sy, ry))[d]
        if m is not None:
            src, dst = chunk(src, d, m), chunk(dst, d, m)
        first[d, m] = remote(src, dst, slot, d, prv[d])
        slot += 1
    for d in range(3):
        src, dst = ((qt, pt), (qz, pz), (qy, py))[d]
        for m in others(d):
            second[d, m] = remote(chunk(src, d, m), chunk(dst, d, m), slot, d, nxt[d])
            slot += 1

    pl.semaphore_wait(barrier, 6)
    for copy in first.values():
        copy.start()
    last_rows.wait()

    def matrix(m, h):
        return [[[load(m, part, i, j, h) for j in range(3)] for i in range(3)] for part in range(2)]

    def save(ref, index, value):
        for part in range(2):
            for i in range(len(value[part])):
                for j in range(3):
                    ref[index, part, i, j] = value[part][i][j]

    def saved(ref, index, rows=3):
        return [[[ref[index, part, i, j] for j in range(3)] for i in range(rows)] for part in range(2)]

    def rolled(m, d, h, part, i, j):
        v = load(m, part, i, j, h)
        if d == 3:
            return jnp.where(g.xcol == NX - 1, g.lanes(v, NX - 1), g.lanes(v, -1))
        if d == 2:
            return g.lanes(v, -NX)
        if d == 1:
            return g.rows(v, -1)
        if h + 1 < halves:
            beyond = g.rows(load(m, part, i, j, h + 1), -depth)
            return jnp.where(g.row >= SUB - depth, beyond, g.rows(v, -depth))
        return g.rows(v, -depth)

    def complete(d, h):
        return d == 3 or (d == 0 and h + 1 < halves)

    slots = {}
    for mu, nu in PLANES:
        for h in range(halves):
            for m, d in ((nu, mu), (mu, nu)):
                slots[m, d, h] = len(slots)
                rows = 3 if complete(d, h) else 2
                save(
                    ahead_s, slots[m, d, h],
                    [[[rolled(m, d, h, part, i, j) for j in range(3)] for i in range(rows)] for part in range(2)],
                )
            save(
                local_s, PLANES.index((mu, nu)) * halves + h,
                product(matrix(mu, h), matrix(nu, h), left_h=True),
            )

    def ahead(m, d, h):
        if complete(d, h):
            return saved(ahead_s, slots[m, d, h])
        index = {c: n for n, c in enumerate(all_comps(d))}

        def get(part, i, j):
            v = ahead_s[slots[m, d, h], part, i, j]
            c = index[(m, part, i, j)]
            if d == 0:
                r = c // g.per * SUB
                edge = g.rows(rt[r : r + SUB, :], SUB - depth - depth * (c % g.per))
                return jnp.where(g.row >= SUB - depth, edge, v)
            if d == 1:
                r = (c // depth * halves + h) * SUB
                edge = g.rows(rz[r : r + SUB, :], depth - 1 - c % depth)
                return jnp.where(g.zrow == depth - 1, edge, v)
            r = (c // g.ygroups * halves + h) * SUB
            edge = g.lanes(ry[r : r + SUB, :], LANES - NX - NX * (c % g.ygroups))
            return jnp.where(g.lane >= LANES - NX, edge, v)

        real = [[get(0, i, j) for j in range(3)] for i in range(2)]
        imag = [[get(1, i, j) for j in range(3)] for i in range(2)]
        third_r, third_i = third_row(real, imag)
        return [real + [third_r], imag + [third_i]]

    seen = set()

    def add(m, c, h, value):
        r = ((m * 8 + c) * halves + h) * SUB
        if (m, c, h) in seen:
            acc[r : r + SUB, :] += value
        else:
            seen.add((m, c, h))
            acc[r : r + SUB, :] = value

    def lower(m, d, h, q):
        base = others(d).index(m) * 8
        if d == 2:
            for c0 in range(0, 8, g.ygroups):
                value = None
                for k in range(g.ygroups):
                    x = g.lanes(q[c0 + k], NX * (k + 1))
                    value = x if value is None else jnp.where(g.lane >= NX * k, x, value)
                r = ((base + c0) // g.ygroups * halves + h) * SUB
                qy[r : r + SUB, :] = value
        elif d == 1:
            for c0 in range(0, 8, depth):
                value = None
                for k in range(depth):
                    x = g.rows(q[c0 + k], k + 1 - depth)
                    value = x if value is None else jnp.where(g.zrow >= k, x, value)
                r = ((base + c0) // depth * halves + h) * SUB
                qz[r : r + SUB, :] = value
        elif d == 0 and h + 1 == halves:
            for c0 in range(0, 8, g.per):
                value = None
                for k in range(g.per):
                    x = g.rows(q[c0 + k], depth * (k + 1))
                    value = x if value is None else jnp.where(g.row >= depth * k, x, value)
                r = (base + c0) // g.per * SUB
                qt[r : r + SUB, :] = value
        for c in range(8):
            if d == 3:
                add(m, c, h, jnp.where(g.xcol == 0, g.lanes(q[c], 1 - NX), g.lanes(q[c], 1)))
            elif d == 2:
                add(m, c, h, jnp.where(g.lane >= NX, g.lanes(q[c], NX), 0.0))
            elif d == 1:
                add(m, c, h, jnp.where(g.zrow > 0, g.rows(q[c], 1), 0.0))
            else:
                moved = g.rows(q[c], depth)
                add(m, c, h, jnp.where(g.row >= depth, moved, 0.0))
                if h + 1 < halves:
                    add(m, c, h + 1, jnp.where(g.row < depth, moved, 0.0))

    waits = {(0, 3): [(0, 3)], (1, 3): [(1, 3)], (0, 2): [(0, 2), (2, None)], (1, 2): [(1, 2)], (0, 1): [(0, 1), (1, 0)]}
    for n, (mu, nu) in enumerate(PLANES):
        for h in range(halves):
            if h == (halves - 1 if (mu, nu) == (0, 3) else 0):
                for key in waits.get((mu, nu), ()):
                    first[key].wait_recv()
            a = product(ahead(nu, mu, h), ahead(mu, nu, h), right_h=True)
            save(plaq_s, n * halves + h, a)
            b = saved(local_s, n * halves + h)
            lower(mu, nu, h, projected(a, b, left_h=True))
            lower(nu, mu, h, projected(a, b, right_h=True))
        for key in ((mu, nu), (nu, mu)):
            if key in second:
                second[key].start()

    for n, (mu, nu) in enumerate(PLANES):
        for h in range(halves):
            e = product(matrix(mu, h), saved(plaq_s, n * halves + h))
            upper = projected(e, matrix(nu, h), right_h=True)
            for c in range(8):
                add(mu, c, h, upper[c])
                add(nu, c, h, -upper[c])

    for m in (2, 0, 1, 3):
        for d in others(m):
            if d < 3:
                second[d, m].wait_recv()
        for h in range(halves):
            for c in range(8):
                r = ((m * 8 + c) * halves + h) * SUB
                value = acc[r : r + SUB, :]
                for d in others(m):
                    b = others(d).index(m) * 8 + c
                    if d == 0 and h == 0:
                        s = b // g.per * SUB
                        x = g.rows(pt[s : s + SUB, :], -depth * (b % g.per))
                        value = value + jnp.where(g.row < depth, x, 0.0)
                    elif d == 1:
                        s = (b // depth * halves + h) * SUB
                        x = g.rows(pz[s : s + SUB, :], -(b % depth))
                        value = value + jnp.where(g.zrow == 0, x, 0.0)
                    elif d == 2:
                        s = (b // g.ygroups * halves + h) * SUB
                        x = g.lanes(py[s : s + SUB, :], -NX * (b % g.ygroups))
                        value = value + jnp.where(g.lane < NX, x, 0.0)
                acc[r : r + SUB, :] = value
    for copy in list(first.values()) + list(second.values()):
        copy.wait_send()


def expand(halves, acc, hbm, out, sems):
    copies = []
    for m in range(4):
        for h in range(halves):
            rows = [((m * 8 + c) * halves + h) * SUB for c in range(8)]
            f = [acc[r : r + SUB, :] * (COEFF * 0.5 if c < 6 else COEFF) for c, r in enumerate(rows)]

            def put(part, i, j, value):
                out[m, part, i, j, h * SUB : (h + 1) * SUB, :] = value

            for n, (i, j) in enumerate(((0, 1), (0, 2), (1, 2))):
                put(0, i, j, f[n])
                put(0, j, i, -f[n])
                put(1, i, j, f[3 + n])
                put(1, j, i, f[3 + n])
            for i in range(3):
                put(0, i, i, jnp.zeros((SUB, LANES), jnp.float32))
            put(1, 0, 0, f[6])
            put(1, 1, 1, f[7])
            put(1, 2, 2, -(f[6] + f[7]))
        copies.append(pltpu.make_async_copy(out.at[m], hbm.at[m], sems.at[m]))
        copies[-1].start()
    for copy in copies:
        copy.wait()


def per_device(counts, links):
    time_len, depth, flat = links.shape[4:]
    sites = time_len * depth
    assert flat == LANES and SUB % depth == 0 and sites % SUB == 0
    halves = sites // SUB
    rows1, rows2 = sizes(depth, halves)
    vmem = lambda *s: pltpu.VMEM(s + (LANES,), jnp.float32)
    shape = links.shape[:4] + (sites, flat)
    terms = pl.pallas_call(
        functools.partial(force_terms, counts, depth, halves),
        out_shape=pltpu.VMEM((32 * sites, flat), jnp.float32),
        in_specs=[pl.BlockSpec(memory_space=pl.ANY)],
        out_specs=pl.BlockSpec(memory_space=pltpu.VMEM),
        scratch_shapes=[
            vmem(*shape[:-1]),
            vmem(12 * halves, 2, 3, 3, SUB),
            vmem(6 * halves, 2, 3, 3, SUB),
            vmem(6 * halves, 2, 3, 3, SUB),
        ]
        + [vmem(r) for r in rows1 + rows1 + rows2 + rows2]
        + [
            pltpu.SemaphoreType.DMA((5,)),
            pltpu.SemaphoreType.DMA((16,)),
            pltpu.SemaphoreType.DMA((16,)),
        ],
        compiler_params=pltpu.CompilerParams(collective_id=0, has_side_effects=True),
        name="force_terms",
    )(links.reshape(shape))
    out = pl.pallas_call(
        functools.partial(expand, halves),
        out_shape=jax.ShapeDtypeStruct(shape, jnp.float32),
        in_specs=[pl.BlockSpec(memory_space=pltpu.VMEM)],
        out_specs=pl.BlockSpec(memory_space=pl.ANY),
        scratch_shapes=[vmem(*shape[:-1]), pltpu.SemaphoreType.DMA((4,))],
        name="expand",
    )(pltpu.with_memory_space_constraint(terms, pltpu.VMEM))
    return out.reshape(links.shape)


def solution(mesh):
    assert mesh.axis_names == ("gx", "gz", "ta")
    counts = tuple(mesh.shape[a] for a in AXES)
    spec = P(None, None, None, None, "ta", "gz", "gx")
    return jax.shard_map(
        functools.partial(per_device, counts),
        mesh=mesh,
        in_specs=(spec,),
        out_specs=spec,
        check_vma=False,
    )
```

time: 18.5 us -> 15.4 us (0.83)
  local copies, waits for them, and re-layouts: 1.92 us -> 0 us
  Pallas kernels: 16.4 us -> 15.3 us
    unnamed x1 -> x0, local copies, waits for them, and re-layouts: 1.92 us -> none
    pallas_call x1 -> x2, Pallas kernels: 16.4 us -> 15.3 us  [the longest x1 14.4 us: per_device(): pl.pallas_call(functools.partial(force_terms, counts, depth, halves), out...]
where the time goes in v2:
time: 15.4 us; the launch traced here: 15.3 us
  Pallas kernels  15.3 us (99%)
    pallas_call x1, Pallas kernels, per_device(): pl.pallas_call(functools.partial(force_terms, counts, depth, halves), out...  14.4 us
    pallas_call x1, Pallas kernels, per_device(): pl.pallas_call(functools.partial(expand, halves), out_shape=jax.ShapeDtyp...  0.86 us

profile of v2, /device:TPU:0, one launch (start us, length us, event | category | flops | bytes accessed | tf_op | source)
XLA Modules:
  0.0 15.3 jit_solution(2482591637857982646)
XLA Ops:
  0.0 14.4 %force_terms.1.acc = f32[512,128]{1,0:T(8,128)S(1)} custom-call(f32[4,2,3,3,16,128]{5,4,3,2,1,0:T(8,128)} %bitcast.2), custom_call_target="tpu_custom_call" | custom-call | tf_op jit(solution)/shard_map/force_terms/pallas_call | solution.py:425
  14.4 0.9 %expand.1 = f32[4,2,3,3,16,128]{5,4,3,2,1,0:T(8,128)} custom-call(f32[512,128]{1,0:T(8,128)S(1)} %force_terms.1.acc), custom_call_target="tpu_custom_call" | custom-call | tf_op jit(solution)/shard_map/expand/pallas_call | solution.py:445

commit v3 on v2

--- a/solution.py
+++ b/solution.py
@@ -107,7 +107,7 @@
     return rows(36), rows(24)
 
 
-PLANES = ((0, 3), (1, 3), (0, 2), (1, 2), (0, 1), (2, 3))
+PLANES = ((2, 3), (1, 3), (1, 2), (0, 3), (0, 2), (0, 1))
 
 
 def force_terms(
@@ -204,7 +204,7 @@
 
     first, second = {}, {}
     slot = 0
-    for d, m in ((0, 3), (1, 3), (2, None), (0, 2), (1, 2), (0, 1), (1, 0)):
+    for d, m in ((0, 3), (0, 2), (0, 1), (1, 3), (1, 2), (1, 0), (2, None)):
         src, dst = ((st, rt), (sz, rz), (sy, ry))[d]
         if m is not None:
             src, dst = chunk(src, d, m), chunk(dst, d, m)
@@ -338,20 +338,26 @@
                 if h + 1 < halves:
                     add(m, c, h + 1, jnp.where(g.row < depth, moved, 0.0))
 
-    waits = {(0, 3): [(0, 3)], (1, 3): [(1, 3)], (0, 2): [(0, 2), (2, None)], (1, 2): [(1, 2)], (0, 1): [(0, 1), (1, 0)]}
-    for n, (mu, nu) in enumerate(PLANES):
-        for h in range(halves):
-            if h == (halves - 1 if (mu, nu) == (0, 3) else 0):
-                for key in waits.get((mu, nu), ()):
-                    first[key].wait_recv()
-            a = product(ahead(nu, mu, h), ahead(mu, nu, h), right_h=True)
-            save(plaq_s, n * halves + h, a)
-            b = saved(local_s, n * halves + h)
-            lower(mu, nu, h, projected(a, b, left_h=True))
-            lower(nu, mu, h, projected(a, b, right_h=True))
+    steps = [(pair, h) for pair in PLANES if pair[0] for h in range(halves)]
+    steps += [(pair, h) for h in range(halves) for pair in PLANES if not pair[0]]
+    arrived, left = set(), {key: halves for key in second}
+    for (mu, nu), h in steps:
+        n = PLANES.index((mu, nu))
+        for d, m in ((mu, nu), (nu, mu)):
+            key = (d, None if d == 2 else m)
+            if key in first and key not in arrived and not complete(d, h):
+                arrived.add(key)
+                first[key].wait_recv()
+        a = product(ahead(nu, mu, h), ahead(mu, nu, h), right_h=True)
+        save(plaq_s, n * halves + h, a)
+        b = saved(local_s, n * halves + h)
+        lower(mu, nu, h, projected(a, b, left_h=True))
+        lower(nu, mu, h, projected(a, b, right_h=True))
         for key in ((mu, nu), (nu, mu)):
             if key in second:
-                second[key].start()
+                left[key] -= 1
+                if not left[key]:
+                    second[key].start()
 
     for n, (mu, nu) in enumerate(PLANES):
         for h in range(halves):
@@ -361,9 +367,9 @@
                 add(mu, c, h, upper[c])
                 add(nu, c, h, -upper[c])
 
-    for m in (2, 0, 1, 3):
+    for m in (3, 2, 1, 0):
         for d in others(m):
-            if d < 3:
+            if d in (1, 2):
                 second[d, m].wait_recv()
         for h in range(halves):
             for c in range(8):
@@ -371,11 +377,7 @@
                 value = acc[r : r + SUB, :]
                 for d in others(m):
                     b = others(d).index(m) * 8 + c
-                    if d == 0 and h == 0:
-                        s = b // g.per * SUB
-                        x = g.rows(pt[s : s + SUB, :], -depth * (b % g.per))
-                        value = value + jnp.where(g.row < depth, x, 0.0)
-                    elif d == 1:
+                    if d == 1:
                         s = (b // depth * halves + h) * SUB
                         x = g.rows(pz[s : s + SUB, :], -(b % depth))
                         value = value + jnp.where(g.zrow == 0, x, 0.0)
@@ -384,6 +386,14 @@
                         x = g.lanes(py[s : s + SUB, :], -NX * (b % g.ygroups))
                         value = value + jnp.where(g.lane < NX, x, 0.0)
                 acc[r : r + SUB, :] = value
+    for m in (3, 2, 1):
+        second[0, m].wait_recv()
+        for c in range(8):
+            r = (m * 8 + c) * halves * SUB
+            b = others(0).index(m) * 8 + c
+            s = b // g.per * SUB
+            x = g.rows(pt[s : s + SUB, :], -depth * (b % g.per))
+            acc[r : r + SUB, :] += jnp.where(g.row < depth, x, 0.0)
     for copy in list(first.values()) + list(second.values()):
         copy.wait_send()
 

time: 15.4 us -> 14.9 us (0.968)
  Pallas kernels: 15.3 us -> 14.7 us
    pallas_call x1, Pallas kernels: 14.4 us -> 13.9 us  [per_device(): pl.pallas_call(functools.partial(force_terms, counts, depth, halves), out...]
where the time goes in v3:
time: 14.9 us; the launch traced here: 14.7 us
  Pallas kernels  14.7 us (99%)
    pallas_call x1, Pallas kernels, per_device(): pl.pallas_call(functools.partial(force_terms, counts, depth, halves), out...  13.9 us
    pallas_call x1, Pallas kernels, per_device(): pl.pallas_call(functools.partial(expand, halves), out_shape=jax.ShapeDtyp...  0.86 us

profile of v3, /device:TPU:0, one launch (start us, length us, event | category | flops | bytes accessed | tf_op | source)
XLA Modules:
  0.0 14.7 jit_solution(12444257869594761885)
XLA Ops:
  0.0 13.9 %force_terms.1.acc = f32[512,128]{1,0:T(8,128)S(1)} custom-call(f32[4,2,3,3,16,128]{5,4,3,2,1,0:T(8,128)} %bitcast.2), custom_call_target="tpu_custom_call" | custom-call | tf_op jit(solution)/shard_map/force_terms/pallas_call | solution.py:435
  13.9 0.9 %expand.1 = f32[4,2,3,3,16,128]{5,4,3,2,1,0:T(8,128)} custom-call(f32[512,128]{1,0:T(8,128)S(1)} %force_terms.1.acc), custom_call_target="tpu_custom_call" | custom-call | tf_op jit(solution)/shard_map/expand/pallas_call | solution.py:455

commit v4 on v3

--- a/solution.py
+++ b/solution.py
@@ -112,7 +112,7 @@
 
 def force_terms(
     counts, depth, halves, hbm, acc,
-    u, ahead_s, local_s, plaq_s, st, sz, sy, rt, rz, ry, qt, qz, qy, pt, pz, py,
+    u, ahead_s, local_s, plaq_s, st, sz, sy, rt, rz, ry, qz, qy, pz, py, bs, br, ezs, ezr, eys, eyr,
     load_sem, send, recv,
 ):
     g = Lattice(depth)
@@ -126,7 +126,18 @@
         by = dict(zip(AXES, where))
         return (by["gx"], by["gz"], by["ta"])
 
+    def diagonal(time, i, index):
+        where = list(me)
+        where[0], where[i] = time, index
+        by = dict(zip(AXES, where))
+        return (by["gx"], by["gz"], by["ta"])
+
     barrier = pltpu.get_barrier_semaphore()
+    for i in (1, 2):
+        for where in (diagonal(nxt[0], i, prv[i]), diagonal(prv[0], i, nxt[i])):
+            pl.semaphore_signal(
+                barrier, inc=1, device_id=where, device_id_type=pl.DeviceIdType.MESH
+            )
     for i in range(3):
         for index in (nxt[i], prv[i]):
             pl.semaphore_signal(
@@ -183,13 +194,41 @@
                 r = (c0 // g.ygroups * halves + h) * SUB
                 sy[r : r + SUB, :] = value
 
+    def pack_back(m):
+        cs = comps(0, m)
+        for c0 in range(0, 12, g.per):
+            value = None
+            for k in range(g.per):
+                x = g.rows(load(*cs[c0 + k], halves - 1), depth * (k + 1))
+                value = x if value is None else jnp.where(g.row >= depth * k, x, value)
+            r = (12 * m + c0) // g.per * SUB
+            bs[r : r + SUB, :] = value
+
+    def pack_edges():
+        cs = comps(0, 0)
+        for c0 in range(0, 12, SUB):
+            rows = lanes = None
+            for k in range(min(SUB, 12 - c0)):
+                v = load(*cs[c0 + k], halves - 1)
+                x = g.rows(v, k - (SUB - depth))
+                rows = x if rows is None else jnp.where(g.row >= k, x, rows)
+            ezs[c0 : c0 + SUB, :] = rows
+        for c0 in range(0, 12, g.ygroups):
+            for k in range(min(g.ygroups, 12 - c0)):
+                x = g.lanes(g.rows(load(*cs[c0 + k], halves - 1), depth), NX * k)
+                lanes = x if k == 0 else jnp.where(g.lane >= NX * k, x, lanes)
+            r = c0 // g.ygroups * SUB
+            eys[r : r + SUB, :] = lanes
+
     for m in (3, 2, 1, 0):
         loads[m].wait()
+        pack_back(m)
         if m != 0:
             pack_t(m)
         if m != 1:
             pack_z(m)
     pack_y()
+    pack_edges()
 
     def remote(src, dst, slot, i, index):
         return pltpu.make_async_remote_copy(
@@ -210,14 +249,25 @@
             src, dst = chunk(src, d, m), chunk(dst, d, m)
         first[d, m] = remote(src, dst, slot, d, prv[d])
         slot += 1
-    for d in range(3):
-        src, dst = ((qt, pt), (qz, pz), (qy, py))[d]
+    back = {}
+    for m in range(4):
+        n = bs.shape[0] // 4
+        back[m] = remote(bs.at[m * n : (m + 1) * n], br.at[m * n : (m + 1) * n], slot, 0, nxt[0])
+        slot += 1
+    for i, src, dst in ((1, ezs, ezr), (2, eys, eyr)):
+        back["edge", i] = pltpu.make_async_remote_copy(
+            src_ref=src, dst_ref=dst, send_sem=send.at[slot], recv_sem=recv.at[slot],
+            device_id=diagonal(nxt[0], i, prv[i]), device_id_type=pl.DeviceIdType.MESH,
+        )
+        slot += 1
+    for d in (1, 2):
+        src, dst = (None, (qz, pz), (qy, py))[d]
         for m in others(d):
             second[d, m] = remote(chunk(src, d, m), chunk(dst, d, m), slot, d, nxt[d])
             slot += 1
 
-    pl.semaphore_wait(barrier, 6)
-    for copy in first.values():
+    pl.semaphore_wait(barrier, 10)
+    for copy in list(first.values()) + [back[k] for k in (("edge", 1), ("edge", 2), 0, 3, 2, 1)]:
         copy.start()
     last_rows.wait()
 
@@ -317,14 +367,6 @@
                     value = x if value is None else jnp.where(g.zrow >= k, x, value)
                 r = ((base + c0) // depth * halves + h) * SUB
                 qz[r : r + SUB, :] = value
-        elif d == 0 and h + 1 == halves:
-            for c0 in range(0, 8, g.per):
-                value = None
-                for k in range(g.per):
-                    x = g.rows(q[c0 + k], depth * (k + 1))
-                    value = x if value is None else jnp.where(g.row >= depth * k, x, value)
-                r = (base + c0) // g.per * SUB
-                qt[r : r + SUB, :] = value
         for c in range(8):
             if d == 3:
                 add(m, c, h, jnp.where(g.xcol == 0, g.lanes(q[c], 1 - NX), g.lanes(q[c], 1)))
@@ -367,6 +409,45 @@
                 add(mu, c, h, upper[c])
                 add(nu, c, h, -upper[c])
 
+    def complete_rows(get):
+        real = [[get(0, i, j) for j in range(3)] for i in range(2)]
+        imag = [[get(1, i, j) for j in range(3)] for i in range(2)]
+        third_r, third_i = third_row(real, imag)
+        return [real + [third_r], imag + [third_i]]
+
+    def behind(m):
+        def get(part, i, j):
+            c = 12 * m + part * 6 + i * 3 + j
+            r = c // g.per * SUB
+            return g.rows(br[r : r + SUB, :], -depth * (c % g.per))
+
+        return complete_rows(get)
+
+    for key in (("edge", 1), ("edge", 2), 0):
+        back[key].wait_recv()
+    time_link = behind(0)
+    for m in (3, 2, 1):
+        back[m].wait_recv()
+
+        def step(part, i, j):
+            v = time_link[part][i][j]
+            c = part * 6 + i * 3 + j
+            if m == 3:
+                return jnp.where(g.xcol == NX - 1, g.lanes(v, NX - 1), g.lanes(v, -1))
+            if m == 1:
+                r = c // SUB * SUB
+                edge = g.rows(ezr[r : r + SUB, :], depth - 1 - c % SUB)
+                return jnp.where(g.row == depth - 1, edge, g.rows(v, -1))
+            r = c // g.ygroups * SUB
+            edge = g.lanes(eyr[r : r + SUB, :], LANES - NX - NX * (c % g.ygroups))
+            return jnp.where(g.lane >= LANES - NX, edge, g.lanes(v, -NX))
+
+        a = product(matrix(m, 0), complete_rows(step), right_h=True)
+        b = product(time_link, behind(m), left_h=True)
+        q = projected(a, b, right_h=True)
+        for c in range(8):
+            add(m, c, 0, jnp.where(g.row < depth, q[c], 0.0))
+
     for m in (3, 2, 1, 0):
         for d in others(m):
             if d in (1, 2):
@@ -386,15 +467,7 @@
                         x = g.lanes(py[s : s + SUB, :], -NX * (b % g.ygroups))
                         value = value + jnp.where(g.lane < NX, x, 0.0)
                 acc[r : r + SUB, :] = value
-    for m in (3, 2, 1):
-        second[0, m].wait_recv()
-        for c in range(8):
-            r = (m * 8 + c) * halves * SUB
-            b = others(0).index(m) * 8 + c
-            s = b // g.per * SUB
-            x = g.rows(pt[s : s + SUB, :], -depth * (b % g.per))
-            acc[r : r + SUB, :] += jnp.where(g.row < depth, x, 0.0)
-    for copy in list(first.values()) + list(second.values()):
+    for copy in list(first.values()) + list(back.values()) + list(second.values()):
         copy.wait_send()
 
 
@@ -443,11 +516,12 @@
             vmem(6 * halves, 2, 3, 3, SUB),
             vmem(6 * halves, 2, 3, 3, SUB),
         ]
-        + [vmem(r) for r in rows1 + rows1 + rows2 + rows2]
+        + [vmem(r) for r in rows1 + rows1 + rows2[1:] + rows2[1:]]
+        + [vmem(r) for r in (rows1[0] // 3 * 4,) * 2 + (2 * SUB,) * 4]
         + [
             pltpu.SemaphoreType.DMA((5,)),
-            pltpu.SemaphoreType.DMA((16,)),
-            pltpu.SemaphoreType.DMA((16,)),
+            pltpu.SemaphoreType.DMA((19,)),
+            pltpu.SemaphoreType.DMA((19,)),
         ],
         compiler_params=pltpu.CompilerParams(collective_id=0, has_side_effects=True),
         name="force_terms",

time: 14.9 us -> 14.8 us (level)
  no operation moved by 1% of the time
where the time goes in v4:
time: 14.8 us; the launch traced here: 14.6 us
  Pallas kernels  14.6 us (99%)
    pallas_call x1, Pallas kernels, per_device(): pl.pallas_call(functools.partial(force_terms, counts, depth, halves), out...  13.8 us
    pallas_call x1, Pallas kernels, per_device(): pl.pallas_call(functools.partial(expand, halves), out_shape=jax.ShapeDtyp...  0.86 us

profile of v4, /device:TPU:0, one launch (start us, length us, event | category | flops | bytes accessed | tf_op | source)
XLA Modules:
  0.0 14.6 jit_solution(3303051938364725311)
XLA Ops:
  0.0 13.8 %force_terms.1.acc = f32[512,128]{1,0:T(8,128)S(1)} custom-call(f32[4,2,3,3,16,128]{5,4,3,2,1,0:T(8,128)} %bitcast.2), custom_call_target="tpu_custom_call" | custom-call | tf_op jit(solution)/shard_map/force_terms/pallas_call | solution.py:508
  13.8 0.9 %expand.1 = f32[4,2,3,3,16,128]{5,4,3,2,1,0:T(8,128)} custom-call(f32[512,128]{1,0:T(8,128)S(1)} %force_terms.1.acc), custom_call_target="tpu_custom_call" | custom-call | tf_op jit(solution)/shard_map/expand/pallas_call | solution.py:529

commit v5 on v4

--- a/solution.py
+++ b/solution.py
@@ -107,7 +107,7 @@
     return rows(36), rows(24)
 
 
-PLANES = ((2, 3), (1, 3), (1, 2), (0, 3), (0, 2), (0, 1))
+PLANES = ((2, 3), (1, 3), (1, 2), (0, 1), (0, 2), (0, 3))
 
 
 def force_terms(
@@ -243,7 +243,7 @@
 
     first, second = {}, {}
     slot = 0
-    for d, m in ((0, 3), (0, 2), (0, 1), (1, 3), (1, 2), (1, 0), (2, None)):
+    for d, m in ((0, 1), (0, 2), (0, 3), (1, 3), (1, 2), (1, 0), (2, None)):
         src, dst = ((st, rt), (sz, rz), (sy, ry))[d]
         if m is not None:
             src, dst = chunk(src, d, m), chunk(dst, d, m)
@@ -267,8 +267,23 @@
             slot += 1
 
     pl.semaphore_wait(barrier, 10)
-    for copy in list(first.values()) + [back[k] for k in (("edge", 1), ("edge", 2), 0, 3, 2, 1)]:
-        copy.start()
+    for key, copy in first.items():
+        if key[0]:
+            copy.start()
+    low_faces = [copy for key, copy in first.items() if not key[0]]
+    high_faces = [back[key] for key in (("edge", 1), ("edge", 2), 0, 3, 2, 1)]
+    around = me[0] == counts[0] - 1
+
+    @pl.when(around)
+    def _():
+        for copy in high_faces + low_faces:
+            copy.start()
+
+    @pl.when(jnp.logical_not(around))
+    def _():
+        for copy in low_faces + high_faces:
+            copy.start()
+
     last_rows.wait()
 
     def matrix(m, h):

time: 14.8 us -> 14.4 us (0.973)
  Pallas kernels: 14.6 us -> 14.3 us
    pallas_call x1, Pallas kernels: 13.8 us -> 13.4 us  [per_device(): pl.pallas_call(functools.partial(force_terms, counts, depth, halves), out...]
where the time goes in v5:
time: 14.4 us; the launch traced here: 14.3 us
  Pallas kernels  14.3 us (99%)
    pallas_call x1, Pallas kernels, per_device(): pl.pallas_call(functools.partial(force_terms, counts, depth, halves), out...  13.4 us
    pallas_call x1, Pallas kernels, per_device(): pl.pallas_call(functools.partial(expand, halves), out_shape=jax.ShapeDtyp...  0.86 us

profile of v5, /device:TPU:0, one launch (start us, length us, event | category | flops | bytes accessed | tf_op | source)
XLA Modules:
  0.0 14.3 jit_solution(12570588577540397695)
XLA Ops:
  0.0 13.4 %force_terms.1.acc = f32[512,128]{1,0:T(8,128)S(1)} custom-call(f32[4,2,3,3,16,128]{5,4,3,2,1,0:T(8,128)} %bitcast.2), custom_call_target="tpu_custom_call" | custom-call | tf_op jit(solution)/shard_map/force_terms/pallas_call | solution.py:523
  13.4 0.9 %expand.1 = f32[4,2,3,3,16,128]{5,4,3,2,1,0:T(8,128)} custom-call(f32[512,128]{1,0:T(8,128)S(1)} %force_terms.1.acc), custom_call_target="tpu_custom_call" | custom-call | tf_op jit(solution)/shard_map/expand/pallas_call | solution.py:544

commit v6 on v5

--- a/solution.py
+++ b/solution.py
@@ -438,32 +438,7 @@
 
         return complete_rows(get)
 
-    for key in (("edge", 1), ("edge", 2), 0):
-        back[key].wait_recv()
-    time_link = behind(0)
-    for m in (3, 2, 1):
-        back[m].wait_recv()
-
-        def step(part, i, j):
-            v = time_link[part][i][j]
-            c = part * 6 + i * 3 + j
-            if m == 3:
-                return jnp.where(g.xcol == NX - 1, g.lanes(v, NX - 1), g.lanes(v, -1))
-            if m == 1:
-                r = c // SUB * SUB
-                edge = g.rows(ezr[r : r + SUB, :], depth - 1 - c % SUB)
-                return jnp.where(g.row == depth - 1, edge, g.rows(v, -1))
-            r = c // g.ygroups * SUB
-            edge = g.lanes(eyr[r : r + SUB, :], LANES - NX - NX * (c % g.ygroups))
-            return jnp.where(g.lane >= LANES - NX, edge, g.lanes(v, -NX))
-
-        a = product(matrix(m, 0), complete_rows(step), right_h=True)
-        b = product(time_link, behind(m), left_h=True)
-        q = projected(a, b, right_h=True)
-        for c in range(8):
-            add(m, c, 0, jnp.where(g.row < depth, q[c], 0.0))
-
-    for m in (3, 2, 1, 0):
+    def add_faces(m):
         for d in others(m):
             if d in (1, 2):
                 second[d, m].wait_recv()
@@ -482,6 +457,36 @@
                         x = g.lanes(py[s : s + SUB, :], -NX * (b % g.ygroups))
                         value = value + jnp.where(g.lane < NX, x, 0.0)
                 acc[r : r + SUB, :] = value
+
+    for m in (3, 2, 1):
+        add_faces(m)
+
+    for key in (("edge", 1), ("edge", 2), 0):
+        back[key].wait_recv()
+    time_link = behind(0)
+    for m in (3, 2, 1):
+        back[m].wait_recv()
+
+        def step(part, i, j):
+            v = time_link[part][i][j]
+            c = part * 6 + i * 3 + j
+            if m == 3:
+                return jnp.where(g.xcol == NX - 1, g.lanes(v, NX - 1), g.lanes(v, -1))
+            if m == 1:
+                r = c // SUB * SUB
+                edge = g.rows(ezr[r : r + SUB, :], depth - 1 - c % SUB)
+                return jnp.where(g.row == depth - 1, edge, g.rows(v, -1))
+            r = c // g.ygroups * SUB
+            edge = g.lanes(eyr[r : r + SUB, :], LANES - NX - NX * (c % g.ygroups))
+            return jnp.where(g.lane >= LANES - NX, edge, g.lanes(v, -NX))
+
+        a = product(matrix(m, 0), complete_rows(step), right_h=True)
+        b = product(time_link, behind(m), left_h=True)
+        q = projected(a, b, right_h=True)
+        for c in range(8):
+            add(m, c, 0, jnp.where(g.row < depth, q[c], 0.0))
+
+    add_faces(0)
     for copy in list(first.values()) + list(back.values()) + list(second.values()):
         copy.wait_send()
 

time: 14.4 us -> 14.6 us (1.014)
  Pallas kernels: 14.3 us -> 14.5 us
    pallas_call x1, Pallas kernels: 13.4 us -> 13.6 us  [per_device(): pl.pallas_call(functools.partial(force_terms, counts, depth, halves), out...]
where the time goes in v6:
time: 14.6 us; the launch traced here: 14.5 us
  Pallas kernels  14.5 us (99%)
    pallas_call x1, Pallas kernels, per_device(): pl.pallas_call(functools.partial(force_terms, counts, depth, halves), out...  13.6 us
    pallas_call x1, Pallas kernels, per_device(): pl.pallas_call(functools.partial(expand, halves), out_shape=jax.ShapeDtyp...  0.86 us

profile of v6, /device:TPU:0, one launch (start us, length us, event | category | flops | bytes accessed | tf_op | source)
XLA Modules:
  0.0 14.5 jit_solution(9218639537837786568)
XLA Ops:
  0.0 13.6 %force_terms.1.acc = f32[512,128]{1,0:T(8,128)S(1)} custom-call(f32[4,2,3,3,16,128]{5,4,3,2,1,0:T(8,128)} %bitcast.2), custom_call_target="tpu_custom_call" | custom-call | tf_op jit(solution)/shard_map/force_terms/pallas_call | solution.py:528
  13.6 0.9 %expand.1 = f32[4,2,3,3,16,128]{5,4,3,2,1,0:T(8,128)} custom-call(f32[512,128]{1,0:T(8,128)S(1)} %force_terms.1.acc), custom_call_target="tpu_custom_call" | custom-call | tf_op jit(solution)/shard_map/expand/pallas_call | solution.py:549
